TPU v7x, 32 devices: a whole 2x2x4 slice. The times are simulated.
32 devices in a mesh: shot: 8 (over z, y), depth: 4 (over x, core).
Axes of the slice: x: 2, y: 2, z: 4, core: 2. Of those that a mesh axis runs over, the one named last changes fastest.
Arguments:
- correlation: float32 [16, 16, 32, 512], P('shot', None, None, 'depth'), may hold values from -6 to 6
- illumination: float32 [16, 16, 32, 512], P('shot', None, None, 'depth'), may hold values from 0.25 to 4
- aperture: int32 [16, 4], P('shot'), may hold values from 0 to 32, as said below
Outputs:
- stack: float32 [16, 32, 512], P('shot', None, 'depth')
Inputs may be any that keep to these rules, and one draw needn't show every extreme that they name: For every shot, 0 <= aperture[s,0] < aperture[s,1] <= 16 and 0 <= aperture[s,2] < aperture[s,3] <= 32; each box spans a quarter to a half of the grid along each of the two dimensions.
All inputs are finite; a program needn't handle non-finite values.
Results may differ from a plain program's by a relative error of at most 0.0003.
Values sent between devices are 32-bit elements.
A program may use at most 64 MiB of HBM per device.

v0:
```python
import math

import jax
import jax.numpy as jnp
from jax import lax
from jax.sharding import PartitionSpec as P


def padded_2(block, sides, width):
    for axis, dim in sides:
        count = lax.axis_size(axis)
        forward = [(i, i + 1) for i in range(count - 1)]
        backward = [(target, source) for source, target in forward]
        low = lax.ppermute(
            lax.slice_in_dim(block, block.shape[dim] - width, None, axis=dim), axis, forward
        )
        high = lax.ppermute(lax.slice_in_dim(block, 0, width, axis=dim), axis, backward)
        block = jnp.concatenate([low, block, high], axis=dim)
    return block


def on_device(correlation, illumination, aperture):
    shots, rows, cols, slab = correlation.shape
    first = lax.broadcasted_iota(jnp.int32, (1, rows, cols, 1), 1)
    second = lax.broadcasted_iota(jnp.int32, (1, rows, cols, 1), 2)
    bounds = aperture.reshape(shots, 4, 1, 1, 1)
    inside = (
        (first >= bounds[:, 0])
        & (first < bounds[:, 1])
        & (second >= bounds[:, 2])
        & (second < bounds[:, 3])
    )
    normalized = inside.astype(jnp.float32) * correlation / (illumination + 0.1)
    padded = padded_2(normalized, (("depth", 3),), 1)
    padded = jnp.pad(padded, ((0, 0), (1, 1), (1, 1), (0, 0)))
    beside = padded[:, 2:, 1:-1, 1:-1] + padded[:, :-2, 1:-1, 1:-1]
    beside = beside + padded[:, 1:-1, 2:, 1:-1] + padded[:, 1:-1, :-2, 1:-1]
    beside = beside + padded[:, 1:-1, 1:-1, 2:] + padded[:, 1:-1, 1:-1, :-2]
    filtered = 6.0 * normalized - beside
    local_energy = jnp.sum(filtered * filtered, axis=(1, 2, 3))
    cells = rows * cols * slab * lax.axis_size("depth")
    total_shots = shots * lax.axis_size("shot")
    meansq = lax.psum(local_energy, "depth") / cells
    peak = lax.pmax(jnp.max(meansq), "shot")
    weight = 1.0 / jnp.sqrt(meansq + 0.5 * peak + 1.0)
    weighted = jnp.sum(weight.reshape(shots, 1, 1, 1) * filtered, axis=0) / math.sqrt(total_shots)
    return lax.psum_scatter(weighted, "shot", scatter_dimension=0, tiled=True)


def solution(mesh):
    return jax.shard_map(
        on_device,
        mesh=mesh,
        in_specs=(P("shot", None, None, "depth"), P("shot", None, None, "depth"), P("shot", None)),
        out_specs=P("shot", None, "depth"),
        check_vma=False,
    )
```

profile of v0, /device:TPU:0, one launch (start us, length us, event | category | flops | bytes accessed | tf_op | source)
XLA Modules:
  0.0 121.8 jit_solution(7367261136840748524)
XLA Ops:
  6.5 0.0 reduce-scatter.2.cloned.1.call-start
  6.5 1.0 slice_reduce_fusion.3
  7.6 0.1 fusion.9
  7.7 1.4 %add_divide_fusion = f32[2,16,32,128]{3,2,1,0:T(8,128)S(1)} fusion(f32[2,16,32,128]{3,2,1,0:T(8,128)} %param.4, f32[2,16,32,128]{3,2,1,0:T(8,128)} %param.3, f32[2,16,32]{2,1,0:T(8,128)S(1)} %fusion.9), kind=kLoop, calls=%fused_computation.19 | loop fusion | flops 393216 | bytes 1576960 | tf_op jit(solution)/shard_map/div | solution.py:33
  9.1 0.2 fusion.11
  9.3 1.3 %collective-permute-start.1 = (f32[2,16,32,1]{3,2,1,0:T(8,128)S(1)}, f32[2,16,32,1]{3,2,1,0:T(8,128)S(1)}, u32[]{:S(2)}, u32[]{:S(2)}) collective-permute-start(f32[2,16,32,1]{3,2,1,0:T(8,128)S(1)} %get-tuple-element.11), channel_id=1, source_target_pairs={{1,0},{2,1},{3,2},{5,4},{6,5},{7,6},{9,8},{10,9},{11,10},{13,12},{... | collective-permute-start | bytes 12296 | tf_op jit(solution)/shard_map/ppermute | solution.py:17
  10.6 3.1 %collective-permute-start = (f32[2,16,32,1]{3,2,1,0:T(8,128)S(1)}, f32[2,16,32,1]{3,2,1,0:T(8,128)S(1)}, u32[]{:S(2)}, u32[]{:S(2)}) collective-permute-start(f32[2,16,32,1]{3,2,1,0:T(8,128)S(1)} %get-tuple-element.12), channel_id=1, source_target_pairs={{0,1},{1,2},{2,3},{4,5},{5,6},{6,7},{8,9},{9,10},{10,11},{12,13},{... | collective-permute-start | bytes 12296 | tf_op jit(solution)/shard_map/ppermute | solution.py:14
  13.7 0.0 collective-permute-done.1
  13.7 1.5 %collective-permute-done = f32[2,16,32,1]{3,2,1,0:T(8,128)S(1)} collective-permute-done((f32[2,16,32,1]{3,2,1,0:T(8,128)S(1)}, f32[2,16,32,1]{3,2,1,0:T(8,128)S(1)}, u32[]{:S(2)}, u32[]{:S(2)}) %collective-permute-start) | collective-permute-done | bytes 4128 | tf_op jit(solution)/shard_map/ppermute | solution.py:14
  15.1 0.6 select_maximum_fusion
  15.7 1.1 multiply_reduce_fusion.1
  16.8 13.1 %psum.7 = f32[2]{0:T(128)S(1)} all-reduce(f32[2]{0:T(128)S(1)} %get-tuple-element.9), channel_id=1, replica_groups=mesh['shot'=8,'depth'=4] {'depth'}, use_global_device_ids=true, to_apply=%region_1.2 | all-reduce | flops 2 | bytes 16 | tf_op jit(solution)/shard_map/psum | solution.py:43
  29.9 0.6 multiply_reduce_fusion.2
  30.5 22.3 %pmax.7 = f32[]{:T(128)} all-reduce(f32[]{:T(128)} %multiply_reduce_fusion.2), channel_id=1, replica_groups=mesh['shot'=8,'depth'=4] {'shot'}, use_global_device_ids=true, to_apply=%region_3.4 | all-reduce | flops 1 | bytes 8 | tf_op jit(solution)/shard_map/pmax | solution.py:44
  53.5 0.1 multiply_reduce_fusion
  53.6 0.7 broadcast_multiply_fusion
  54.3 0.0 reduce-scatter.2.cloned.1.call-update
  54.3 60.6 %reduce-scatter.2.cloned.1.call-done = f32[2,32,128]{2,1,0:T(8,128)} async-done(((f32[16,32,128]{2,1,0:T(8,128)}), f32[2,32,128]{2,1,0:T(8,128)}) %reduce-scatter.2.cloned.1.call-update) | async-done | bytes 32784 | tf_op jit(solution)/shard_map/reduce_scatter | solution.py:47
  (1 shorter events, 0.0 us)
Async XLA Ops:
  6.5 108.4 %reduce-scatter.2.cloned.1.call-start = ((), (), s32[]{:S(2)}) async-start(), calls=%async_computation.1 | async-start | bytes 294912 | tf_op jit(solution)/shard_map/reduce_scatter | solution.py:47
  9.3 4.4 %collective-permute-start.1 = (f32[2,16,32,1]{3,2,1,0:T(8,128)S(1)}, f32[2,16,32,1]{3,2,1,0:T(8,128)S(1)}, u32[]{:S(2)}, u32[]{:S(2)}) collective-permute-start(f32[2,16,32,1]{3,2,1,0:T(8,128)S(1)} %get-tuple-element.11), channel_id=1, source_target_pairs={{1,0},{2,1},{3,2},{5,4},{6,5},{7,6},{9,8},{10,9},{11,10},{13,12},{... | collective-permute-start | bytes 12296 | tf_op jit(solution)/shard_map/ppermute | solution.py:17
  10.6 4.6 %collective-permute-start = (f32[2,16,32,1]{3,2,1,0:T(8,128)S(1)}, f32[2,16,32,1]{3,2,1,0:T(8,128)S(1)}, u32[]{:S(2)}, u32[]{:S(2)}) collective-permute-start(f32[2,16,32,1]{3,2,1,0:T(8,128)S(1)} %get-tuple-element.12), channel_id=1, source_target_pairs={{0,1},{1,2},{2,3},{4,5},{5,6},{6,7},{8,9},{9,10},{10,11},{12,13},{... | collective-permute-start | bytes 12296 | tf_op jit(solution)/shard_map/ppermute | solution.py:14
Sparse Core Ops, SparseCore 0:
  54.4 60.4 reduce-scatter.1
where the time goes:
time: 122 us
  waiting for transfers between devices  62.1 us (51%)
  blocking collectives  35.4 us (29%)
  between operations  14.1 us (12%)
  other arithmetic  4.62 us (4%)
  starting transfers between devices  4.36 us (4%)
  local copies, waits for them, and re-layouts  1.25 us (1%)
    reduce_scatter x1, waiting for transfers between devices, on_device(): return lax.psum_scatter(weighted, 'shot', scatter_dimension=0, tiled=True)  60.6 us
    pmax x1, blocking collectives, on_device(): peak = lax.pmax(jnp.max(meansq), 'shot')  22.3 us
    psum x1, blocking collectives, on_device(): meansq = lax.psum(local_energy, 'depth') / cells  13.1 us
    ppermute x1, starting transfers between devices, padded_2(): lax.ppermute(lax.slice_in_dim(block, block.shape[dim] - width, None, axis...  3.06 us
  transfers between devices with their start and end apart: 3, of which 2 were waited for; matrix products, arithmetic and copies ran while one was open for 0% of the time, Pallas kernels for 0%

commit v1 on v0

v1 whole, which is shorter than its diff:
```python
import functools
import math

import jax
import jax.numpy as jnp
from jax import lax
from jax.experimental import pallas as pl
from jax.experimental.pallas import tpu as pltpu
from jax.sharding import PartitionSpec as P

MESH = pl.DeviceIdType.MESH
LANES = 128
SUBLANES = 8


def kernel(dims, corr_hbm, ill_hbm, box, out_ref, corr, ill, norm, halo_out, halo_in, send, recv,
           energy_out, energy_in, note_out, note_in, load_sem, halo_sem, bulk_send, bulk_recv,
           energy_send, energy_recv, note_send, note_recv):
    shots, rows, cols, slab, groups, slabs, owned, width, total_shots, cells = dims
    tiles = cols // SUBLANES
    per_row = shots * tiles
    rows_per_pack = LANES // per_row
    packs = rows // rows_per_pack
    group = lax.axis_index("shot")
    depth = lax.axis_index("depth")

    loads = []
    for s in range(shots):
        pair = (
            pltpu.make_async_copy(corr_hbm.at[s], corr.at[s], load_sem.at[0, s]),
            pltpu.make_async_copy(ill_hbm.at[s], ill.at[s], load_sem.at[1, s]),
        )
        for copy in pair:
            copy.start()
        loads.append(pair)

    barrier = pltpu.get_barrier_semaphore()
    for j in range(1, slabs):
        pl.semaphore_signal(barrier, inc=1, device_id={"depth": lax.rem(depth + j, slabs)}, device_id_type=MESH)
    for j in range(1, groups):
        pl.semaphore_signal(barrier, inc=1, device_id={"shot": lax.rem(group + j, groups)}, device_id_type=MESH)

    lane = lax.broadcasted_iota(jnp.int32, (SUBLANES, LANES), 1)
    lane_row = lax.broadcasted_iota(jnp.int32, (cols, slab), 1)
    col = lax.broadcasted_iota(jnp.int32, (cols, slab), 0)
    plane = jnp.zeros((cols, slab), jnp.float32)
    edge = jnp.zeros((SUBLANES, slab), jnp.float32)
    for s in range(shots):
        norm[s, 0, pl.ds(SUBLANES, cols)] = plane
        norm[s, rows + 1, pl.ds(SUBLANES, cols)] = plane

    col_mask = [(col >= box[s, 2]) & (col < box[s, 3]) for s in range(shots)]
    for pair in loads:
        for copy in pair:
            copy.wait()

    def normalise(p, carry):
        low = edge
        high = edge
        for i in range(rows_per_pack):
            r = p * rows_per_pack + i
            for s in range(shots):
                inside = col_mask[s] & (r >= box[s, 0]) & (r < box[s, 1])
                value = jnp.where(inside, corr[s, r], 0.0) / (ill[s, r] + 0.1)
                norm[s, r + 1, pl.ds(0, SUBLANES)] = edge
                norm[s, r + 1, pl.ds(SUBLANES, cols)] = value
                norm[s, r + 1, pl.ds(SUBLANES + cols, SUBLANES)] = edge
                for c in range(tiles):
                    k = (i * shots + s) * tiles + c
                    piece = value[c * SUBLANES:(c + 1) * SUBLANES]
                    low = jnp.where(lane == k, pltpu.roll(piece, k, 1), low)
                    high = jnp.where(lane == k, pltpu.roll(piece, (k + 1) % LANES, 1), high)
        halo_out[0, p] = low
        halo_out[1, p] = high
        return carry

    lax.fori_loop(0, packs, normalise, 0)

    pl.semaphore_wait(barrier, slabs + groups - 2)

    halos = []
    for side, step in ((0, slabs - 1), (1, 1)):
        copy = pltpu.make_async_remote_copy(
            src_ref=halo_out.at[side], dst_ref=halo_in.at[side],
            send_sem=halo_sem.at[0, side], recv_sem=halo_sem.at[1, side],
            device_id={"depth": lax.rem(depth + step, slabs)}, device_id_type=MESH)
        copy.start()
        halos.append(copy)
    for copy in halos:
        copy.wait()

    fold_mask = col < cols - width
    has_high = depth < slabs - 1
    has_low = depth > 0

    def filtered(p, energies):
        energies = list(energies)
        from_high = jnp.where(has_high, halo_in[0, p], 0.0)
        from_low = jnp.where(has_low, halo_in[1, p], 0.0)
        for i in range(rows_per_pack):
            r = p * rows_per_pack + i
            owner = p * (rows_per_pack // owned) + i // owned
            for s in range(shots):
                lows = []
                highs = []
                for c in range(tiles):
                    k = (i * shots + s) * tiles + c
                    lows.append(pltpu.roll(from_low, (LANES - k) % LANES, 1))
                    highs.append(pltpu.roll(from_high, LANES - 1 - k, 1))
                value = norm[s, r + 1, pl.ds(SUBLANES, cols)]
                beside = norm[s, r + 2, pl.ds(SUBLANES, cols)] + norm[s, r, pl.ds(SUBLANES, cols)]
                beside = beside + norm[s, r + 1, pl.ds(SUBLANES + 1, cols)]
                beside = beside + norm[s, r + 1, pl.ds(SUBLANES - 1, cols)]
                before = jnp.where(lane_row == 0, jnp.concatenate(lows, axis=0), pltpu.roll(value, 1, 1))
                after = jnp.where(lane_row == slab - 1, jnp.concatenate(highs, axis=0), pltpu.roll(value, slab - 1, 1))
                result = 6.0 * value - (beside + before + after)
                energies[s] = energies[s] + result * result
                other = pltpu.roll(result, cols - width, 0)
                folded = result + jnp.where(fold_mask, other, 0.0)
                send[owner, pl.ds((s * owned + i % owned) * width, width)] = folded[:width]
        return tuple(energies)

    energies = lax.fori_loop(0, packs, filtered, (plane,) * shots)

    order = sorted(range(1, groups), key=lambda j: abs(2 * j - groups))
    bulk = {}
    for j in order:
        target = lax.rem(group + j, groups)
        copy = pltpu.make_async_remote_copy(
            src_ref=send.at[target], dst_ref=recv.at[j - 1],
            send_sem=bulk_send.at[j - 1], recv_sem=bulk_recv.at[j - 1],
            device_id={"shot": target}, device_id_type=MESH)
        copy.start()
        bulk[j] = copy

    def total(value):
        return jnp.sum(jnp.sum(value, axis=0, keepdims=True), axis=1, keepdims=True)

    shot_row = lax.broadcasted_iota(jnp.int32, note_out.shape, 0)
    message = jnp.zeros(note_out.shape, jnp.float32)
    for s in range(shots):
        message = jnp.where(shot_row == s, total(energies[s]), message)
    energy_out[...] = message
    copies = []
    for j in range(1, slabs):
        copy = pltpu.make_async_remote_copy(
            src_ref=energy_out, dst_ref=energy_in.at[j - 1],
            send_sem=energy_send.at[j - 1], recv_sem=energy_recv.at[j - 1],
            device_id={"depth": lax.rem(depth + j, slabs)}, device_id_type=MESH)
        copy.start()
        copies.append(copy)
    for j, copy in enumerate(copies):
        copy.wait()
        message = message + energy_in[j]
    message = message / cells
    for s in range(shots):
        message = jnp.where(shot_row == shots + s, (box[s, 2] - 1).astype(jnp.float32), message)
    note_out[...] = message
    notes = {}
    for j in order:
        copy = pltpu.make_async_remote_copy(
            src_ref=note_out, dst_ref=note_in.at[j - 1],
            send_sem=note_send.at[j - 1], recv_sem=note_recv.at[j - 1],
            device_id={"shot": lax.rem(group + j, groups)}, device_id_type=MESH)
        copy.start()
        notes[j] = copy
    for j in order:
        notes[j].wait()
    peak = jnp.where(shot_row < shots, message, 0.0)
    for j in range(1, groups):
        peak = jnp.maximum(peak, jnp.where(shot_row < shots, note_in[j - 1], 0.0))
    peak = jnp.max(peak, axis=0, keepdims=True)

    scale = 1.0 / math.sqrt(total_shots)
    col_float = col.astype(jnp.float32)

    def unfold(block, note, sums):
        weight = scale / jnp.sqrt(note + 0.5 * peak + 1.0)
        for s in range(shots):
            first = note[shots + s:shots + s + 1]
            inside = (col_float >= first) & (col_float < first + width)
            factor = jnp.where(inside, weight[s:s + 1], 0.0)
            for i in range(owned):
                value = block[pl.ds((s * owned + i) * width, width)]
                sums[i] = sums[i] + factor * jnp.concatenate([value, value[:cols - width]], axis=0)
        return sums

    sums = unfold(send.at[group], message, [plane] * owned)
    for j in reversed(order):
        bulk[j].wait()
        sums = unfold(recv.at[j - 1], note_in[j - 1], sums)
    for i in range(owned):
        out_ref[i] = sums[i]


def on_device(correlation, illumination, aperture):
    shots, rows, cols, slab = correlation.shape
    groups = lax.axis_size("shot")
    slabs = lax.axis_size("depth")
    owned = rows // groups
    width = min(cols, cols // 2 + 2)
    dims = (shots, rows, cols, slab, groups, slabs, owned, width, shots * groups, rows * cols * slab * slabs)
    packs = rows * shots * (cols // SUBLANES) // LANES
    note_rows = -(-2 * shots // SUBLANES) * SUBLANES
    block = (shots * owned * width, slab)
    f32 = jnp.float32
    dma = pltpu.SemaphoreType.DMA
    return pl.pallas_call(
        functools.partial(kernel, dims),
        out_shape=jax.ShapeDtypeStruct((owned, cols, slab), f32),
        in_specs=[
            pl.BlockSpec(memory_space=pl.ANY),
            pl.BlockSpec(memory_space=pl.ANY),
            pl.BlockSpec(memory_space=pltpu.SMEM),
        ],
        out_specs=pl.BlockSpec(memory_space=pltpu.VMEM),
        scratch_shapes=[
            pltpu.VMEM((shots, rows, cols, slab), f32),
            pltpu.VMEM((shots, rows, cols, slab), f32),
            pltpu.VMEM((shots, rows + 2, cols + 2 * SUBLANES, slab), f32),
            pltpu.VMEM((2, packs, SUBLANES, LANES), f32),
            pltpu.VMEM((2, packs, SUBLANES, LANES), f32),
            pltpu.VMEM((groups,) + block, f32),
            pltpu.VMEM((groups - 1,) + block, f32),
            pltpu.VMEM((note_rows, LANES), f32),
            pltpu.VMEM((slabs - 1, note_rows, LANES), f32),
            pltpu.VMEM((note_rows, LANES), f32),
            pltpu.VMEM((groups - 1, note_rows, LANES), f32),
            dma((2, shots)),
            dma((2, 2)),
            dma((groups - 1,)),
            dma((groups - 1,)),
            dma((slabs - 1,)),
            dma((slabs - 1,)),
            dma((groups - 1,)),
            dma((groups - 1,)),
        ],
        compiler_params=pltpu.CompilerParams(collective_id=0, has_side_effects=True),
    )(correlation, illumination, aperture)


def solution(mesh):
    return jax.shard_map(
        on_device,
        mesh=mesh,
        in_specs=(P("shot", None, None, "depth"), P("shot", None, None, "depth"), P("shot", None)),
        out_specs=P("shot", None, "depth"),
        check_vma=False,
    )
```

time: 122 us -> 21.2 us (0.17)
  waiting for transfers between devices: 62.1 us -> 0 us
  blocking collectives: 35.4 us -> 0 us
  Pallas kernels: 0 us -> 19.6 us
  between operations: 14.1 us -> 0.01 us
  other arithmetic: 4.62 us -> 0 us
  starting transfers between devices: 4.36 us -> 0 us
    reduce_scatter x1 -> x0, waiting for transfers between devices: 60.6 us -> none  [on_device(): return lax.psum_scatter(weighted, 'shot', scatter_dimension=0, tiled=True)]
    pmax x1 -> x0, blocking collectives: 22.3 us -> none  [on_device(): peak = lax.pmax(jnp.max(meansq), 'shot')]
    pallas_call x0 -> x1, Pallas kernels: none -> 19.6 us  [on_device(): pl.pallas_call(functools.partial(kernel, dims), out_shape=jax.ShapeDtypeS...]
    psum x1 -> x0, blocking collectives: 13.1 us -> none  [on_device(): meansq = lax.psum(local_energy, 'depth') / cells]
    ppermute x2 -> x0, starting transfers between devices: 4.36 us -> none  [the longest x1 3.06 us: padded_2(): lax.ppermute(lax.slice_in_dim(block, block.shape[dim] - width, None, axis...]
    div x2 -> x0, other arithmetic: 2.12 us -> none  [the longest x1 1.41 us: on_device(): normalized = inside.astype(jnp.float32) * correlation / (illumination + 0.1)]
    ppermute x2 -> x0, waiting for transfers between devices: 1.48 us -> none  [the longest x1 1.48 us: padded_2(): lax.ppermute(lax.slice_in_dim(block, block.shape[dim] - width, None, axis...]
    unnamed x0 -> x1, local copies, waits for them, and re-layouts: none -> 1.38 us
  transfers between devices with their start and end apart: 3 -> 0, of which waited for: 2 -> 0; matrix products, arithmetic and copies ran while one was open for 0% -> 0% of each run, Pallas kernels for 0% -> 0%
where the time goes in v1:
time: 21.2 us; the launch traced here: 21 us
  Pallas kernels  19.6 us (92%)
  local copies, waits for them, and re-layouts  1.38 us (7%)
    pallas_call x1, Pallas kernels, on_device(): pl.pallas_call(functools.partial(kernel, dims), out_shape=jax.ShapeDtypeS...  19.6 us
    unnamed x1, local copies, waits for them, and re-layouts  1.38 us

profile of v1, /device:TPU:0, one launch (start us, length us, event | category | flops | bytes accessed | tf_op | source)
XLA Modules:
  0.0 21.0 jit_solution(2695847955612278195)
XLA Ops:
  0.0 19.6 %shard_map.37 = f32[2,32,128]{2,1,0:T(8,128)} custom-call(f32[2,16,32,128]{3,2,1,0:T(8,128)} %corr_hbm.1, f32[2,16,32,128]{3,2,1,0:T(8,128)} %ill_hbm.1, s32[2,4]{1,0:T(2,128)} %box.1), custom_call_target="tpu_custom_call" | custom-call | tf_op jit(solution)/shard_map/pallas_call | solution.py:208
  19.6 1.4 %copy.5 = f32[2,32,128]{2,1,0:T(8,128)} copy(f32[2,32,128]{2,1,0:T(8,128)} %shard_map.37) | data formatting | bytes 65536

commit v2 on v1

v2 whole, which is shorter than its diff:
```python
import functools
import math

import jax
import jax.numpy as jnp
from jax import lax
from jax.experimental import pallas as pl
from jax.experimental.pallas import tpu as pltpu
from jax.sharding import PartitionSpec as P

MESH = pl.DeviceIdType.MESH
LANES = 128
SUBLANES = 8
AHEAD = None


def kernel(dims, corr_hbm, ill_hbm, box, out_ref, corr, ill, norm, edge_out, edge_in, send, recv,
           note_out, note_in, load_sem, edge_send, edge_recv, bulk_send, bulk_recv, note_send, note_recv):
    shots, rows, cols, slab, groups, slabs, owned, width, total_shots, cells = dims
    tiles = cols // SUBLANES
    per_row = shots * tiles
    rows_per_pack = LANES // per_row
    packs = rows // rows_per_pack
    per_owner = owned * per_row
    owners_per_pack = LANES // per_owner
    group = lax.axis_index("shot")
    depth = lax.axis_index("depth")

    barrier = pltpu.get_barrier_semaphore()
    for j in range(1, groups):
        pl.semaphore_signal(barrier, inc=1, device_id={"shot": lax.rem(group + j, groups)}, device_id_type=MESH)
    for j in range(1, slabs):
        pl.semaphore_signal(barrier, inc=1, device_id={"depth": lax.rem(depth + j, slabs)}, device_id_type=MESH)

    loads = []
    for s in range(shots):
        pair = (
            pltpu.make_async_copy(corr_hbm.at[s], corr.at[s], load_sem.at[0, s]),
            pltpu.make_async_copy(ill_hbm.at[s], ill.at[s], load_sem.at[1, s]),
        )
        for copy in pair:
            copy.start()
        loads.append(pair)

    lane = lax.broadcasted_iota(jnp.int32, (SUBLANES, LANES), 1)
    lane_row = lax.broadcasted_iota(jnp.int32, (cols, slab), 1)
    col = lax.broadcasted_iota(jnp.int32, (cols, slab), 0)
    plane = jnp.zeros((cols, slab), jnp.float32)
    edge = jnp.zeros((SUBLANES, slab), jnp.float32)
    for s in range(shots):
        norm[s, 0, pl.ds(SUBLANES, cols)] = plane
        norm[s, rows + 1, pl.ds(SUBLANES, cols)] = plane

    col_mask = [(col >= box[s, 2]) & (col < box[s, 3]) for s in range(shots)]
    for pair in loads:
        for copy in pair:
            copy.wait()

    def pack(value, i, s, low, high):
        for c in range(tiles):
            k = (i * shots + s) * tiles + c
            piece = value[c * SUBLANES:(c + 1) * SUBLANES]
            low = jnp.where(lane == k, pltpu.roll(piece, k, 1), low)
            high = jnp.where(lane == k, pltpu.roll(piece, (k + 1) % LANES, 1), high)
        return low, high

    def normalise(p, carry):
        low = edge
        high = edge
        for i in range(rows_per_pack):
            r = p * rows_per_pack + i
            for s in range(shots):
                inside = col_mask[s] & (r >= box[s, 0]) & (r < box[s, 1])
                value = jnp.where(inside, corr[s, r], 0.0) / (ill[s, r] + 0.1)
                norm[s, r + 1, pl.ds(0, SUBLANES)] = edge
                norm[s, r + 1, pl.ds(SUBLANES, cols)] = value
                norm[s, r + 1, pl.ds(SUBLANES + cols, SUBLANES)] = edge
                low, high = pack(value, i, s, low, high)
        edge_out[p] = low
        edge_out[packs + p] = high
        return carry

    lax.fori_loop(0, packs, normalise, 0)

    fold_mask = col < cols - width
    not_first = lane_row > 0
    not_last = lane_row < slab - 1

    def filtered(p, energies):
        energies = list(energies)
        low = edge
        high = edge
        for i in range(rows_per_pack):
            r = p * rows_per_pack + i
            owner = p * (rows_per_pack // owned) + i // owned
            for s in range(shots):
                value = norm[s, r + 1, pl.ds(SUBLANES, cols)]
                beside = norm[s, r + 2, pl.ds(SUBLANES, cols)] + norm[s, r, pl.ds(SUBLANES, cols)]
                beside = beside + norm[s, r + 1, pl.ds(SUBLANES + 1, cols)]
                beside = beside + norm[s, r + 1, pl.ds(SUBLANES - 1, cols)]
                before = jnp.where(not_first, pltpu.roll(value, 1, 1), 0.0)
                after = jnp.where(not_last, pltpu.roll(value, slab - 1, 1), 0.0)
                result = 6.0 * value - (beside + before + after)
                energies[s] = energies[s] + result * result
                low, high = pack(result, i, s, low, high)
                other = pltpu.roll(result, cols - width, 0)
                folded = result + jnp.where(fold_mask, other, 0.0)
                send[owner, pl.ds((s * owned + i % owned) * width, width)] = folded[:width]
        edge_out[2 * packs + p] = low
        edge_out[3 * packs + p] = high
        return tuple(energies)

    energies = lax.fori_loop(0, packs, filtered, (plane,) * shots)

    def total(value):
        return jnp.sum(jnp.sum(value, axis=0, keepdims=True), axis=1, keepdims=True)

    shot_row = lax.broadcasted_iota(jnp.int32, (SUBLANES, LANES), 0)
    message = edge
    for s in range(shots):
        message = jnp.where(shot_row == s, total(energies[s]), message)
    edge_out[4 * packs] = message

    pl.semaphore_wait(barrier, slabs + groups - 2)

    edges = []
    for j in range(1, slabs):
        copy = pltpu.make_async_remote_copy(
            src_ref=edge_out, dst_ref=edge_in.at[j - 1],
            send_sem=edge_send.at[j - 1], recv_sem=edge_recv.at[j - 1],
            device_id={"depth": lax.rem(depth + j, slabs)}, device_id_type=MESH)
        copy.start()
        edges.append(copy)

    order = sorted(range(1, groups), key=lambda j: abs(2 * j - groups))
    ahead = len(order) if AHEAD is None else min(AHEAD, len(order))
    bulk = {}
    for j in order:
        target = lax.rem(group + j, groups)
        bulk[j] = pltpu.make_async_remote_copy(
            src_ref=send.at[target], dst_ref=recv.at[j - 1],
            send_sem=bulk_send.at[j - 1], recv_sem=bulk_recv.at[j - 1],
            device_id={"shot": target}, device_id_type=MESH)
    for j in order[:ahead]:
        bulk[j].start()

    for copy in edges:
        copy.wait()
    places = [edge_out] + [edge_in.at[slabs - i - 1] for i in range(1, slabs)]
    for i in range(1, slabs):
        message = message + places[i][4 * packs]
    cross = edge
    for i in range(slabs):
        here, there = places[i], places[(i + 1) % slabs]
        part = edge
        for p in range(packs):
            above = there[p]
            below = here[packs + p]
            part = part + above * (above - 2.0 * here[3 * packs + p])
            part = part + below * (below - 2.0 * there[2 * packs + p])
        cross = cross + jnp.where(lax.rem(depth + i, slabs) < slabs - 1, part, 0.0)
    lane_shot = lax.rem(lane // tiles, shots)
    for s in range(shots):
        message = message + jnp.where(shot_row == s, total(jnp.where(lane_shot == s, cross, 0.0)), 0.0)
    message = message / cells
    for s in range(shots):
        message = jnp.where(shot_row == shots + s, (box[s, 2] - 1).astype(jnp.float32), message)
    for p in range(packs):
        low = jnp.where(depth > 0, places[slabs - 1][packs + p], 0.0)
        high = jnp.where(depth < slabs - 1, places[1][p], 0.0)
        for q in range(owners_per_pack):
            offset = q * per_owner
            halo = jnp.where(lane < per_owner, pltpu.roll(low, (LANES - offset) % LANES, 1),
                             pltpu.roll(high, (LANES + per_owner - offset) % LANES, 1))
            owner = p * owners_per_pack + q
            note_out[owner, 0] = jnp.where(lane < 2 * per_owner, halo, 0.0)
            note_out[owner, 1] = message
    notes = {}
    for j in order:
        target = lax.rem(group + j, groups)
        notes[j] = pltpu.make_async_remote_copy(
            src_ref=note_out.at[target], dst_ref=note_in.at[j - 1],
            send_sem=note_send.at[j - 1], recv_sem=note_recv.at[j - 1],
            device_id={"shot": target}, device_id_type=MESH)
        notes[j].start()
    for j in order[ahead:]:
        bulk[j].start()
    for j in order:
        notes[j].wait()
    peak = jnp.where(shot_row < shots, message, 0.0)
    for j in range(1, groups):
        peak = jnp.maximum(peak, jnp.where(shot_row < shots, note_in[j - 1, 1], 0.0))
    peak = jnp.max(peak, axis=0, keepdims=True)

    scale = 1.0 / math.sqrt(total_shots)
    col_float = col.astype(jnp.float32)

    def unfold(block, note, sums):
        row = note[1]
        weight = scale / jnp.sqrt(jnp.where(shot_row < shots, row, 0.0) + 0.5 * peak + 1.0)
        by_lane = edge
        for s in range(shots):
            first = row[shots + s:shots + s + 1]
            inside = (col_float >= first) & (col_float < first + width)
            factor = jnp.where(inside, weight[s:s + 1], 0.0)
            by_lane = jnp.where(lane_shot == s, weight[s:s + 1], by_lane)
            for i in range(owned):
                value = block[pl.ds((s * owned + i) * width, width)]
                sums[i] = sums[i] + factor * jnp.concatenate([value, value[:cols - width]], axis=0)
        sums[owned] = sums[owned] + by_lane * note[0]
        return sums

    sums = unfold(send.at[group], note_out.at[group], [plane] * owned + [edge])
    for j in order[:ahead][::-1] + order[ahead:]:
        bulk[j].wait()
        sums = unfold(recv.at[j - 1], note_in.at[j - 1], sums)
    halo = sums[owned]
    for s in range(1, shots):
        halo = halo + pltpu.roll(sums[owned], LANES - s * tiles, 1)
    for i in range(owned):
        lows = []
        highs = []
        for c in range(tiles):
            k = i * per_row + c
            lows.append(pltpu.roll(halo, (LANES - k) % LANES, 1))
            highs.append(pltpu.roll(halo, LANES - 1 - per_owner - k, 1))
        value = sums[i] - jnp.where(not_first, 0.0, jnp.concatenate(lows, axis=0))
        out_ref[i] = value - jnp.where(not_last, 0.0, jnp.concatenate(highs, axis=0))


def on_device(correlation, illumination, aperture):
    shots, rows, cols, slab = correlation.shape
    groups = lax.axis_size("shot")
    slabs = lax.axis_size("depth")
    owned = rows // groups
    width = min(cols, cols // 2 + 2)
    dims = (shots, rows, cols, slab, groups, slabs, owned, width, shots * groups, rows * cols * slab * slabs)
    packs = rows * shots * (cols // SUBLANES) // LANES
    edges = (4 * packs + 1, SUBLANES, LANES)
    block = (shots * owned * width, slab)
    f32 = jnp.float32
    dma = pltpu.SemaphoreType.DMA
    return pl.pallas_call(
        functools.partial(kernel, dims),
        out_shape=jax.ShapeDtypeStruct((owned, cols, slab), f32),
        in_specs=[
            pl.BlockSpec(memory_space=pl.ANY),
            pl.BlockSpec(memory_space=pl.ANY),
            pl.BlockSpec(memory_space=pltpu.SMEM),
        ],
        out_specs=pl.BlockSpec(memory_space=pltpu.VMEM),
        scratch_shapes=[
            pltpu.VMEM((shots, rows, cols, slab), f32),
            pltpu.VMEM((shots, rows, cols, slab), f32),
            pltpu.VMEM((shots, rows + 2, cols + 2 * SUBLANES, slab), f32),
            pltpu.VMEM(edges, f32),
            pltpu.VMEM((slabs - 1,) + edges, f32),
            pltpu.VMEM((groups,) + block, f32),
            pltpu.VMEM((groups - 1,) + block, f32),
            pltpu.VMEM((groups, 2, SUBLANES, LANES), f32),
            pltpu.VMEM((groups - 1, 2, SUBLANES, LANES), f32),
            dma((2, shots)),
            dma((slabs - 1,)),
            dma((slabs - 1,)),
            dma((groups - 1,)),
            dma((groups - 1,)),
            dma((groups - 1,)),
            dma((groups - 1,)),
        ],
        compiler_params=pltpu.CompilerParams(collective_id=0, has_side_effects=True),
    )(correlation, illumination, aperture)


def solution(mesh):
    return jax.shard_map(
        on_device,
        mesh=mesh,
        in_specs=(P("shot", None, None, "depth"), P("shot", None, None, "depth"), P("shot", None)),
        out_specs=P("shot", None, "depth"),
        check_vma=False,
    )
```

time: 21.2 us -> 20.9 us (0.986)
  Pallas kernels: 19.6 us -> 19.3 us
    pallas_call x1, Pallas kernels: 19.6 us -> 19.3 us  [on_device(): pl.pallas_call(functools.partial(kernel, dims), out_shape=jax.ShapeDtypeS...]
where the time goes in v2:
time: 20.9 us; the launch traced here: 20.7 us
  Pallas kernels  19.3 us (92%)
  local copies, waits for them, and re-layouts  1.38 us (7%)
    pallas_call x1, Pallas kernels, on_device(): pl.pallas_call(functools.partial(kernel, dims), out_shape=jax.ShapeDtypeS...  19.3 us
    unnamed x1, local copies, waits for them, and re-layouts  1.38 us

profile of v2, /device:TPU:0, one launch (start us, length us, event | category | flops | bytes accessed | tf_op | source)
XLA Modules:
  0.0 20.7 jit_solution(12998248290280012585)
XLA Ops:
  0.0 19.3 %shard_map.37 = f32[2,32,128]{2,1,0:T(8,128)} custom-call(f32[2,16,32,128]{3,2,1,0:T(8,128)} %corr_hbm.1, f32[2,16,32,128]{3,2,1,0:T(8,128)} %ill_hbm.1, s32[2,4]{1,0:T(2,128)} %box.1), custom_call_target="tpu_custom_call" | custom-call | tf_op jit(solution)/shard_map/pallas_call | solution.py:243
  19.3 1.4 %copy.5 = f32[2,32,128]{2,1,0:T(8,128)} copy(f32[2,32,128]{2,1,0:T(8,128)} %shard_map.37) | data formatting | bytes 65536

commit v3 on v2

--- a/solution.py
+++ b/solution.py
@@ -11,7 +11,7 @@
 MESH = pl.DeviceIdType.MESH
 LANES = 128
 SUBLANES = 8
-AHEAD = None
+NEAR = 2
 
 
 def kernel(dims, corr_hbm, ill_hbm, box, out_ref, corr, ill, norm, edge_out, edge_in, send, recv,
@@ -133,7 +133,19 @@
         edges.append(copy)
 
     order = sorted(range(1, groups), key=lambda j: abs(2 * j - groups))
-    ahead = len(order) if AHEAD is None else min(AHEAD, len(order))
+    pair = 2 if groups % 2 == 0 else 1
+
+    def distance(j):
+        target = lax.rem(group + j, groups)
+        return jnp.abs(target // pair - group // pair) + jnp.abs(lax.rem(target, pair) - lax.rem(group, pair))
+
+    def start_bulk(far):
+        for level in range(3, -1, -1):
+            if (level >= NEAR) == far:
+                for j in order:
+                    near = distance(j)
+                    pl.when((near > level) & ((near <= level + 1) | (level == 3)))(bulk[j].start)
+
     bulk = {}
     for j in order:
         target = lax.rem(group + j, groups)
@@ -141,8 +153,7 @@
             src_ref=send.at[target], dst_ref=recv.at[j - 1],
             send_sem=bulk_send.at[j - 1], recv_sem=bulk_recv.at[j - 1],
             device_id={"shot": target}, device_id_type=MESH)
-    for j in order[:ahead]:
-        bulk[j].start()
+    start_bulk(True)
 
     for copy in edges:
         copy.wait()
@@ -183,8 +194,7 @@
             send_sem=note_send.at[j - 1], recv_sem=note_recv.at[j - 1],
             device_id={"shot": target}, device_id_type=MESH)
         notes[j].start()
-    for j in order[ahead:]:
-        bulk[j].start()
+    start_bulk(False)
     for j in order:
         notes[j].wait()
     peak = jnp.where(shot_row < shots, message, 0.0)
@@ -211,7 +221,7 @@
         return sums
 
     sums = unfold(send.at[group], note_out.at[group], [plane] * owned + [edge])
-    for j in order[:ahead][::-1] + order[ahead:]:
+    for j in order:
         bulk[j].wait()
         sums = unfold(recv.at[j - 1], note_in.at[j - 1], sums)
     halo = sums[owned]
@@ -242,7 +252,7 @@
     dma = pltpu.SemaphoreType.DMA
     return pl.pallas_call(
         functools.partial(kernel, dims),
-        out_shape=jax.ShapeDtypeStruct((owned, cols, slab), f32),
+        out_shape=pltpu.VMEM((owned, cols, slab), f32),
         in_specs=[
             pl.BlockSpec(memory_space=pl.ANY),
             pl.BlockSpec(memory_space=pl.ANY),

time: 20.9 us -> 18.2 us (0.87)
  Pallas kernels: 19.3 us -> 17.4 us
  local copies, waits for them, and re-layouts: 1.38 us -> 0.62 us
    pallas_call x1, Pallas kernels: 19.3 us -> 17.4 us  [on_device(): pl.pallas_call(functools.partial(kernel, dims), out_shape=pltpu.VMEM((own...]
    unnamed x1, local copies, waits for them, and re-layouts: 1.38 us -> 0.62 us
where the time goes in v3:
time: 18.2 us; the launch traced here: 18 us
  Pallas kernels  17.4 us (96%)
  local copies, waits for them, and re-layouts  0.62 us (3%)
    pallas_call x1, Pallas kernels, on_device(): pl.pallas_call(functools.partial(kernel, dims), out_shape=pltpu.VMEM((own...  17.4 us
    unnamed x1, local copies, waits for them, and re-layouts  0.62 us

profile of v3, /device:TPU:0, one launch (start us, length us, event | category | flops | bytes accessed | tf_op | source)
XLA Modules:
  0.0 18.0 jit_solution(11205764757535413262)
XLA Ops:
  0.0 17.4 %shard_map.37 = f32[2,32,128]{2,1,0:T(8,128)S(1)} custom-call(f32[2,16,32,128]{3,2,1,0:T(8,128)} %corr_hbm.1, f32[2,16,32,128]{3,2,1,0:T(8,128)} %ill_hbm.1, s32[2,4]{1,0:T(2,128)} %box.1), custom_call_target="tpu_custom_call" | custom-call | tf_op jit(solution)/shard_map/pallas_call | solution.py:253
  17.4 0.6 %copy.5 = f32[2,32,128]{2,1,0:T(8,128)} copy(f32[2,32,128]{2,1,0:T(8,128)S(1)} %shard_map.37) | data formatting | bytes 65536

commit v4 on v3

--- a/solution.py
+++ b/solution.py
@@ -193,7 +193,10 @@
             src_ref=note_out.at[target], dst_ref=note_in.at[j - 1],
             send_sem=note_send.at[j - 1], recv_sem=note_recv.at[j - 1],
             device_id={"shot": target}, device_id_type=MESH)
-        notes[j].start()
+    for level in range(3, -1, -1):
+        for j in order:
+            near = distance(j)
+            pl.when((near > level) & ((near <= level + 1) | (level == 3)))(notes[j].start)
     start_bulk(False)
     for j in order:
         notes[j].wait()

time: 18.2 us -> 18.1 us (level)
  no operation moved by 1% of the time
where the time goes in v4:
time: 18.1 us; the launch traced here: 18 us
  Pallas kernels  17.3 us (96%)
  local copies, waits for them, and re-layouts  0.62 us (3%)
    pallas_call x1, Pallas kernels, on_device(): pl.pallas_call(functools.partial(kernel, dims), out_shape=pltpu.VMEM((own...  17.3 us
    unnamed x1, local copies, waits for them, and re-layouts  0.62 us

profile of v4, /device:TPU:0, one launch (start us, length us, event | category | flops | bytes accessed | tf_op | source)
XLA Modules:
  0.0 18.0 jit_solution(2797620974328496222)
XLA Ops:
  0.0 17.3 %shard_map.37 = f32[2,32,128]{2,1,0:T(8,128)S(1)} custom-call(f32[2,16,32,128]{3,2,1,0:T(8,128)} %corr_hbm.1, f32[2,16,32,128]{3,2,1,0:T(8,128)} %ill_hbm.1, s32[2,4]{1,0:T(2,128)} %box.1), custom_call_target="tpu_custom_call" | custom-call | tf_op jit(solution)/shard_map/pallas_call | solution.py:256
  17.3 0.6 %copy.5 = f32[2,32,128]{2,1,0:T(8,128)} copy(f32[2,32,128]{2,1,0:T(8,128)S(1)} %shard_map.37) | data formatting | bytes 65536
